TPU v7x, 32 devices: a whole 2x2x4 slice. The times are simulated.
32 devices in a mesh: gx: 4 (over y, core), gy: 8 (over z, x).
Axes of the slice: x: 2, y: 2, z: 4, core: 2. Of those that a mesh axis runs over, the one named last changes fastest.
Arguments:
- populations: float32 [19, 16, 64, 128], P(None, 'gx', 'gy'), may hold values from 0.004 to 0.8, as said below
- solid: int32 [16, 64, 128], P('gx', 'gy'), may hold values 0 or 1
- base_cell: int32 [3, 4, 8, 2, 768], P(None, 'gx', 'gy'), may hold values from 0 to 127, as said below
- offset: float32 [3, 4, 8, 2, 768], P(None, 'gx', 'gy'), may hold values from 0 to 1
- rest_displacement: float32 [3, 4, 8, 2, 768], P(None, 'gx', 'gy'), may hold values from 0 to 1
- stiffness: float32 [4, 8, 2], P('gx', 'gy'), may hold values from 0.006380062 to 0.063800626
- occupied: int32 [4, 8, 2], P('gx', 'gy'), may hold values from 0 to 1, as said below
- triangles: int32 [1280, 3], replicated, may hold values from 0 to 641, as said below
Outputs:
- populations_out: float32 [19, 16, 64, 128], P(None, 'gx', 'gy')
- offset_out: float32 [3, 4, 8, 2, 768], P(None, 'gx', 'gy')
Inputs may be any that keep to these rules, and one draw needn't show every extreme that they name: `populations`: every entry is positive. `base_cell`: component 0 of a vertex stored at index i of gx lies in [i * 4, (i + 1) * 4), component 1 of one stored at index j of gy lies in [j * 8, (j + 1) * 8), component 2 lies below 128. The occupied slots of a device come first; each device has at least one, and some device has all 2. `triangles`: each row holds three different vertex numbers below 642.
All inputs are finite; a program needn't handle non-finite values. No bound on the sum of `solid` on one device may be relied on, other than what follows from the above.
Results may differ from a plain program's by a relative error of at most 0.0001.
Values sent between devices are 32-bit elements; how exact they have to be, the bound alone decides.
A program may use at most 64 MiB of HBM per device.

v0:
```python
import functools
import math

import jax
import jax.numpy as jnp
from jax import lax
from jax.experimental import pallas as pl
from jax.experimental.pallas import tpu as pltpu
from jax.sharding import PartitionSpec as P

SUBSTEPS = 3
VELOCITIES = [
    (0, 0, 0), (1, 0, 0), (-1, 0, 0), (0, 1, 0), (0, -1, 0), (0, 0, 1), (0, 0, -1),
    (1, 1, 0), (-1, -1, 0), (1, -1, 0), (-1, 1, 0), (1, 0, 1), (-1, 0, -1), (1, 0, -1),
    (-1, 0, 1), (0, 1, 1), (0, -1, -1), (0, 1, -1), (0, -1, 1),
]
OPPOSITE = [0, 2, 1, 4, 3, 6, 5, 8, 7, 10, 9, 12, 11, 14, 13, 16, 15, 18, 17]
LATTICE_WEIGHTS = [1.0 / 3.0] + [1.0 / 18.0] * 6 + [1.0 / 36.0] * 12
RELAX = 0.8
XS = {s: [q for q in range(19) if VELOCITIES[q][0] == s] for s in (1, -1)}
YS = {s: [q for q in range(19) if VELOCITIES[q][1] == s] for s in (1, -1)}
CORNER = {(v[0], v[1]): q for q, v in enumerate(VELOCITIES) if v[0] and v[1]}
DIRS = [(1, 0), (-1, 0), (0, 1), (0, -1), (1, 1), (1, -1), (-1, 1), (-1, -1)]
MESH = pl.DeviceIdType.MESH
NT = (((1,), (1,)), ((), ()))
NN = (((1,), (0,)), ((), ()))


def mm(a, b, dims):
    return lax.dot_general(a, b, dims, preferred_element_type=jnp.float32)


def split(value):
    high = value.astype(jnp.bfloat16)
    low = (value - high.astype(jnp.float32)).astype(jnp.bfloat16)
    return high, low


def quarter_sine(t):
    t = t - 4.0 * jnp.floor(t * 0.25 + 0.5)
    t = jnp.where(t > 1.0, 2.0 - t, jnp.where(t < -1.0, -2.0 - t, t))
    x = t * (math.pi / 2.0)
    u = x * x
    p = 1.0 / 6227020800.0
    for c in (-1.0 / 39916800.0, 1.0 / 362880.0, -1.0 / 5040.0, 1.0 / 120.0, -1.0 / 6.0, 1.0):
        p = p * u + c
    return x * p


def table(rows, base, kernels):
    cells = lax.broadcasted_iota(jnp.int32, (rows, base.shape[1]), 0)
    d = (cells - base + 1) & (rows - 1)
    out = jnp.where(d == 3, kernels[3], 0.0)
    for s in (2, 1, 0):
        out = jnp.where(d == s, kernels[s], out)
    return out


def moments(pops):
    density = functools.reduce(lambda a, b: a + b, pops)
    momentum = []
    for a in range(3):
        plus = [pops[q] for q in range(19) if VELOCITIES[q][a] == 1]
        minus = [pops[q] for q in range(19) if VELOCITIES[q][a] == -1]
        momentum.append(
            functools.reduce(lambda a, b: a + b, plus)
            - functools.reduce(lambda a, b: a + b, minus)
        )
    return density, momentum


def collide(pops, force, walled):
    density, momentum = moments(pops)
    inverse = 1.0 / density
    u = [(momentum[a] + 0.5 * force[a]) * inverse for a in range(3)]
    squared = u[0] * u[0] + u[1] * u[1] + u[2] * u[2]
    working = u[0] * force[0] + u[1] * force[1] + u[2] * force[2]
    base = 1.0 - 1.5 * squared
    relaxed = []
    for q in range(19):
        vector = VELOCITIES[q]
        along, pushed = jnp.zeros_like(density), jnp.zeros_like(density)
        for a in range(3):
            if vector[a] == 1:
                along, pushed = along + u[a], pushed + force[a]
            elif vector[a] == -1:
                along, pushed = along - u[a], pushed - force[a]
        w = LATTICE_WEIGHTS[q]
        equilibrium = (w * density) * (base + along * (3.0 + 4.5 * along))
        source = ((1.0 - 0.5 / RELAX) * w) * (3.0 * (pushed - working) + 9.0 * along * pushed)
        updated = pops[q] - (pops[q] - equilibrium) * (1.0 / RELAX) + source
        relaxed.append(jnp.where(walled, pops[OPPOSITE[q]], updated))
    return relaxed


def roll(x, shift, axis):
    size = x.shape[axis]
    shift = shift % size
    return x if shift == 0 else pltpu.roll(x, shift, axis)


def row_mask(start, rows, depth):
    sub = lax.broadcasted_iota(jnp.int32, (8, depth), 0)
    return ((sub - start) & 7) < rows


def pack(tiles, start, rows):
    per, out = 8 // rows, []
    for g in range(0, len(tiles), per):
        acc = tiles[g]
        for k, tile in enumerate(tiles[g + 1 : g + per], 1):
            mask = row_mask(start + k * rows, rows, tile.shape[1])
            acc = jnp.where(mask, roll(tile, k * rows, 0), acc)
        out.append(acc)
    return out


def unpack(load, count, rows):
    per = 8 // rows
    return [roll(load(k // per), -(k % per) * rows, 0) for k in range(count)]


def packed(count, rows):
    return -(-count // (8 // rows))


def force_planes(sx, rows_x):
    return {1: [rows_x, rows_x + 1], -1: [-1], 0: list(range(rows_x))}[sx]


def moment_planes(sx, rows_x):
    return {1: [rows_x - 1, rows_x], -1: [-1, 0, 1], 0: list(range(-1, rows_x + 1))}[sx]


def landing(x, sx, rows_x):
    return x - sx * rows_x


def force_size(sx, sy, rows_x):
    n = 3 * len(force_planes(sx, rows_x))
    return {0: n, 1: packed(n, 2), -1: packed(n, 1)}[sy]


def moment_size(sx, sy, rows_x):
    n = 4 * len(moment_planes(sx, rows_x))
    return {0: n + packed(n, 2), 1: packed(n, 2), -1: packed(n, 1) + packed(n, 2)}[sy]


def total_of(parts):
    return functools.reduce(lambda a, b: a + b, parts)


def body_kernel(
    peers_x, peers_y,
    pops_ref, solid_ref, base_ref, offset_ref, rest_ref, stiff_ref, occ_ref, tri_ref,
    pops_out, offset_out,
    lap, off, spread, moved_ref, wide,
    *scratch,
):
    recv_force, recv_pops, recv_mom = scratch[0:8], scratch[8:16], scratch[16:24]
    send_force, send_pops, send_mom = scratch[24:32], scratch[32:40], scratch[40:48]
    send_px, send_py, send_pc = send_pops[0:2], send_pops[2:4], send_pops[4:8]
    send_sem, recv_sem, load_sem = scratch[48:51]
    rows_x = pops_ref.shape[1]
    depth = pops_ref.shape[3]
    slots, padded = base_ref.shape[1], base_ref.shape[2]
    vertices = slots * padded
    planes = rows_x + 3
    ix, iy = lax.axis_index("gx"), lax.axis_index("gy")
    peer = [((ix + sx + peers_x) % peers_x, (iy + sy + peers_y) % peers_y) for sx, sy in DIRS]

    load_pops = pltpu.make_async_copy(pops_ref, pops_out, load_sem)
    load_pops.start()
    barrier = pltpu.get_barrier_semaphore()
    for p in peer:
        pl.semaphore_signal(barrier, inc=1, device_id=p, device_id_type=MESH)

    faces = tri_ref.shape[1]
    pairs = None
    for start in range(0, faces, 256):
        stop = min(start + 256, faces)
        ids = lax.broadcasted_iota(jnp.int32, (base_ref.shape[2], stop - start), 0)
        corner = [tri_ref[k : k + 1, start:stop] for k in range(3)]
        hit = (ids == corner[0]) | (ids == corner[1]) | (ids == corner[2])
        part = jnp.where(hit, 1.0, 0.0).astype(jnp.bfloat16)
        part = mm(part, part, NT)
        pairs = part if pairs is None else pairs + part
    same = lax.broadcasted_iota(jnp.int32, pairs.shape, 0) == lax.broadcasted_iota(
        jnp.int32, pairs.shape, 1
    )
    lap_high, lap_low = split(jnp.where(same, -2.0 * pairs, pairs))
    lap[0] = lap_high
    lap[1] = lap_low

    def flat(ref):
        return jnp.concatenate([ref[:, m, :] for m in range(slots)], axis=1)

    base = flat(base_ref)
    base_x = base[0:1] - ix * rows_x
    base_y = base[1:2] - iy * pops_ref.shape[2]
    base_z = base[2:3]
    live = jnp.concatenate(
        [jnp.full((1, padded), occ_ref[m].astype(jnp.float32)) for m in range(slots)], axis=1
    )
    scale = live * jnp.concatenate(
        [jnp.full((1, padded), stiff_ref[m]) for m in range(slots)], axis=1
    )
    off[...] = flat(offset_ref)
    sub = lax.broadcasted_iota(jnp.int32, (8, depth), 0)
    load_pops.wait()

    def copy(step, stage, d, src, dst):
        return pltpu.make_async_remote_copy(
            src_ref=src, dst_ref=dst.at[step], send_sem=send_sem.at[step, stage, d],
            recv_sem=recv_sem.at[step, stage, d], device_id=peer[d], device_id_type=MESH,
        )

    groups = ((send_force, recv_force), (send_mom, recv_mom), (send_pops, recv_pops))

    def copies(step, stage):
        src, dst = groups[stage]
        return [copy(step, stage, d, src[d].at[step], dst[d]) for d in range(8)]

    def launch(step, stage):
        sends = copies(step, stage)

        @pl.when(iy % 2 == 1)
        def _():
            for d in (4, 6, 2, 5, 7, 3, 0, 1):
                sends[d].start()

        @pl.when(iy % 2 == 0)
        def _():
            for d in (5, 7, 3, 4, 6, 2, 0, 1):
                sends[d].start()

    def arrive(step, stage):
        for x in copies(step, stage):
            x.wait_recv()

    def finish_pops(step):
        arrive(step, 2)
        from_y = {1: recv_pops[2][step], -1: recv_pops[3][step]}
        for q in range(19):
            sx, sy, _ = VELOCITIES[q]
            value = moved_ref[q]
            edge_row = sub == (0 if sy == 1 else 7)
            if sy:
                value = jnp.where(edge_row, roll(from_y[sy], -YS[sy].index(q), 1), value)
            if sx:
                side = recv_pops[0 if sx == 1 else 1][step, XS[sx].index(q)]
                if sy:
                    side = jnp.where(edge_row, recv_pops[DIRS.index((sx, sy))][step], side)
                if sx == 1:
                    value = jnp.concatenate([side[None], value[:-1]], axis=0)
                else:
                    value = jnp.concatenate([value[1:], side[None]], axis=0)
            pops_out[q] = value

    def substep(step, carry):
        now = off[...]
        strain = now - flat(rest_ref)
        six = jnp.concatenate(
            [strain[:, m * padded : (m + 1) * padded] for m in range(slots)], axis=0
        )
        six_high = six.astype(jnp.bfloat16).astype(jnp.float32)
        both = jnp.concatenate([six_high, six - six_high], axis=0).astype(jnp.bfloat16)
        pulled = mm(both, lap[0], NN) + mm(both, lap[1], NN)
        pulled = pulled[0 : 3 * slots] + pulled[3 * slots :]
        force_v = scale * jnp.concatenate(
            [pulled[3 * m : 3 * m + 3] for m in range(slots)], axis=1
        )
        s = quarter_sine(now) * 0.25
        c = quarter_sine(now + 1.0) * 0.25
        kernels = (0.25 - s, 0.25 + c, 0.25 + s, 0.25 - c)
        table_x = table(8, base_x, [k[0:1] for k in kernels])
        table_y = table(16, base_y, [k[1:2] for k in kernels])
        deep_high, deep_low = split(table(depth, base_z, [k[2:3] for k in kernels]))
        deep = jnp.concatenate([deep_high, deep_low], axis=0)
        tiles_of = {}

        def spread_tiles(names, start):
            for n in range(0, len(names), 2):
                blocks = [
                    (force_v[a : a + 1] * table_x[x & 7 : (x & 7) + 1])
                    * table_y[8 * t : 8 * t + 8]
                    for x, a, t in names[n : n + 2]
                ]
                high, low = split(jnp.concatenate(blocks, axis=0))
                row = start + 8 * n
                spread[0, row : row + 16, :] = high
                spread[1, row : row + 16, :] = low
            stop = start + 8 * len(names)
            first = mm(spread[0, start:stop], deep, NT)
            total = first[:, :depth] + first[:, depth:]
            total = total + mm(spread[1, start:stop], deep_high, NT)
            for n, name in enumerate(names):
                tiles_of[name] = total[8 * n : 8 * n + 8]

        outer = [(x, a, t) for x in (rows_x, rows_x + 1, -1) for a in range(3) for t in (0, 1)]
        outer += [(x, a, 1) for x in range(rows_x) for a in range(3)]
        spread_tiles(outer, 0)
        for d, (sx, sy) in enumerate(DIRS):
            tiles = [
                tiles_of[x, a, 0 if sy == 0 else 1]
                for x in force_planes(sx, rows_x) for a in range(3)
            ]
            if sy:
                tiles = pack(tiles, 0 if sy == 1 else 7, 2 if sy == 1 else 1)
            for k, tile in enumerate(tiles):
                send_force[d][step, k] = tile
        @pl.when(step == 0)
        def _():
            pl.semaphore_wait(barrier, len(peer))

        launch(step, 0)
        spread_tiles([(x, a, 0) for x in range(rows_x) for a in range(3)], 8 * len(outer))

        @pl.when(step > 0)
        def _():
            finish_pops(step - 1)

        arrive(step, 0)
        parts = {(x, a): [tiles_of[x, a, 0]] for x in range(rows_x) for a in range(3)}
        for d, (sx, sy) in enumerate(DIRS):
            names = [
                (landing(x, sx, rows_x), a) for x in force_planes(sx, rows_x) for a in range(3)
            ]
            load = lambda k, d=d: recv_force[d][step, k]
            if sy == 0:
                tiles = [load(k) for k in range(len(names))]
            else:
                start, rows = (0, 2) if sy == 1 else (7, 1)
                mask = row_mask(start, rows, depth)
                tiles = [jnp.where(mask, t, 0.0) for t in unpack(load, len(names), rows)]
            for name, tile in zip(names, tiles):
                parts[name].append(tile)
        force = [
            jnp.stack([total_of(parts[x, a]) for x in range(rows_x)]) for a in range(3)
        ]

        relaxed = collide([pops_out[q] for q in range(19)], force, solid_ref[...] != 0)
        moved = [
            roll(roll(relaxed[q], VELOCITIES[q][2], 2), VELOCITIES[q][1], 1) for q in range(19)
        ]
        for q in range(19):
            moved_ref[q] = moved[q]
        nothing = jnp.zeros((1, 8, depth), jnp.float32)
        rho, mz = {}, {}
        for cx in (-1, 0, 1):
            for cy in (-1, 0, 1):
                members = [q for q in range(19) if VELOCITIES[q][:2] == (cx, cy)]
                pad = lambda v: jnp.concatenate(
                    [nothing] * (1 + cx) + [v] + [nothing] * (1 - cx), axis=0
                )
                rho[cx, cy] = pad(total_of([moved[q] for q in members]))
                up = [moved[q] for q in members if VELOCITIES[q][2] == 1]
                down = [moved[q] for q in members if VELOCITIES[q][2] == -1]
                if up:
                    mz[cx, cy] = pad(total_of(up) - total_of(down))
        first_row, last_row = sub == 0, sub == 7
        own = {}
        zero = jnp.zeros((rows_x + 2, 8, depth), jnp.float32)
        fields = []
        for cy in (0, 1, -1):
            dens = rho[-1, cy] + rho[0, cy] + rho[1, cy]
            deep_m = [mz[cx, cy] for cx in (-1, 0, 1) if (cx, cy) in mz]
            fields.append((
                dens, rho[1, cy] - rho[-1, cy], zero if cy == 0 else cy * dens, total_of(deep_m)
            ))
        for c in range(4):
            mid, up, down = (fields[g][c] for g in range(3))
            near = mid + jnp.where(first_row, 0.0, up) + jnp.where(last_row, 0.0, down)
            if c:
                half = 0.5 * force[c - 1]
                near = near + jnp.concatenate([nothing, half, nothing], axis=0)
            far = jnp.where(first_row, up, jnp.where(last_row, down, 0.0))
            for x in range(-1, rows_x + 1):
                own[x, c] = (near[x + 1], far[x + 1])
        for d, (sx, sy) in enumerate(DIRS):
            names = [(x, c) for x in moment_planes(sx, rows_x) for c in range(4)]
            near, far = [own[n][0] for n in names], [own[n][1] for n in names]
            if sy == 0:
                tiles = near + pack(far, 7, 2)
            elif sy == 1:
                tiles = pack([jnp.where(last_row, a, b) for a, b in zip(near, far)], 7, 2)
            else:
                tiles = pack(far, 7, 1) + pack(near, 0, 2)
            for k, tile in enumerate(tiles):
                send_mom[d][step, k] = tile
        launch(step, 1)
        for n, sx in enumerate((1, -1)):
            edge = rows_x - 1 if sx == 1 else 0
            for k, q in enumerate(XS[sx]):
                send_px[n][step, k] = moved[q][edge]
        for n, sy in enumerate((1, -1)):
            rows_kept = moved[YS[sy][0]]
            start = 0 if sy == 1 else 7
            for k, q in enumerate(YS[sy][1:], 1):
                rows_kept = jnp.where(sub == (start + k) % 8, roll(moved[q], k, 1), rows_kept)
            send_py[n][step] = rows_kept
        for n, (sx, sy) in enumerate(DIRS[4:]):
            send_pc[n][step] = moved[CORNER[sx, sy]][rows_x - 1 if sx == 1 else 0]
        launch(step, 2)
        arrive(step, 1)
        reach = [x for x in range(rows_x + 2)] + [-1]
        near = {(x, c): [] for x in reach for c in range(4)}
        far = {(x, c): [] for x in reach for c in range(4)}
        for name, (a, b) in own.items():
            near[name].append(a)
            far[name].append(b)
        two, edges, one = row_mask(0, 2, depth), row_mask(7, 2, depth), row_mask(7, 1, depth)
        for d, (sx, sy) in enumerate(DIRS):
            names = [
                (landing(x, sx, rows_x), c)
                for x in moment_planes(sx, rows_x) for c in range(4)
            ]
            count = len(names)
            load = lambda k, d=d: recv_mom[d][step, k]
            if sy == 0:
                a = [load(k) for k in range(count)]
                b = unpack(lambda k: load(count + k), count, 2)
                b = [jnp.where(edges, t, 0.0) for t in b]
            elif sy == 1:
                both_rows = unpack(load, count, 2)
                a = [jnp.where(first_row, t, 0.0) for t in both_rows]
                b = [jnp.where(last_row, t, 0.0) for t in both_rows]
            else:
                skip = packed(count, 1)
                a = [jnp.where(one, t, 0.0) for t in unpack(load, count, 1)]
                b = unpack(lambda k: load(skip + k), count, 2)
                b = [jnp.where(two, t, 0.0) for t in b]
            for name, p, r in zip(names, a, b):
                near[name].append(p)
                far[name].append(r)
        used = row_mask(7, 3, depth)
        for i, x in enumerate(reach):
            for t, side in enumerate((near, far)):
                dens = total_of(side[x, 0])
                if t:
                    dens = jnp.where(used, dens, 1.0)
                inverse = 1.0 / dens
                for a in range(3):
                    wide[i, a, t] = total_of(side[x, a + 1]) * inverse
        wide_high, wide_low = split(wide[...].reshape(planes * 3 * 16, depth))
        twice = jnp.concatenate([wide_high, wide_high], axis=1)
        along = mm(twice, deep, NN) + mm(wide_low, deep_high, NN)
        along = along.reshape(planes, 3, 16, vertices)
        drift, order = [], list(range(rows_x + 2)) + [7]
        for a in range(3):
            acc = along[0, a] * table_x[0:1]
            for i, x in enumerate(order[1:], 1):
                acc = acc + along[i, a] * table_x[x : x + 1]
            drift.append(jnp.sum(acc * table_y, axis=0, keepdims=True))
        off[...] = now + live * jnp.concatenate(drift, axis=0)
        return carry

    lax.fori_loop(0, SUBSTEPS, substep, 0)
    finish_pops(SUBSTEPS - 1)

    for m in range(slots):
        offset_out[:, m, :] = off[:, m * padded : (m + 1) * padded]

    def drain(step, carry):
        for stage in range(3):
            for x in copies(step, stage):
                x.wait_send()
        return carry

    lax.fori_loop(0, SUBSTEPS, drain, 0)


def local(mesh, populations, solid, base_cell, offset, rest, stiffness, occupied, triangles):
    rows_x, rows_y, depth = populations.shape[1:]
    slots, padded = offset.shape[3:]
    assert rows_y == 8 and rows_x == 4 and depth & (depth - 1) == 0
    vertices, planes = slots * padded, rows_x + 3
    S = SUBSTEPS
    f32, bf16 = jnp.float32, jnp.bfloat16
    tile = (8, depth)
    pop_shapes = [(5,)] * 2 + [(rows_x,)] * 2 + [()] * 4
    V = lambda shape, dtype=f32: pltpu.VMEM(shape, dtype)
    scratch = [
        V((2, padded, padded), bf16), V((3, vertices)),
        V((2, planes * 48, vertices), bf16),
        V((19, rows_x) + tile), V((planes, 3, 2) + tile),
    ]
    for _ in ("receive", "send"):
        scratch += [V((S, force_size(*d, rows_x)) + tile) for d in DIRS]
        scratch += [V((S,) + p + tile) for p in pop_shapes]
        scratch += [V((S, moment_size(*d, rows_x)) + tile) for d in DIRS]
    scratch += [pltpu.SemaphoreType.DMA((S, 3, 8)), pltpu.SemaphoreType.DMA((S, 3, 8))]
    scratch += [pltpu.SemaphoreType.DMA(())]
    vmem = pl.BlockSpec(memory_space=pltpu.VMEM)
    smem = pl.BlockSpec(memory_space=pltpu.SMEM)
    small = (3, slots, padded)
    pops, moved = pl.pallas_call(
        functools.partial(body_kernel, mesh.shape["gx"], mesh.shape["gy"]),
        out_shape=(
            jax.ShapeDtypeStruct(populations.shape, f32),
            jax.ShapeDtypeStruct(small, f32),
        ),
        in_specs=[pl.BlockSpec(memory_space=pl.ANY)] + [vmem] * 4 + [smem] * 2 + [vmem],
        out_specs=(vmem, vmem),
        scratch_shapes=scratch,
        compiler_params=pltpu.CompilerParams(
            collective_id=0, has_side_effects=True, vmem_limit_bytes=60 * 1024 * 1024
        ),
    )(
        populations, solid, base_cell.reshape(small), offset.reshape(small), rest.reshape(small),
        stiffness.reshape(slots), occupied.reshape(slots), triangles.T,
    )
    return pops, moved.reshape(offset.shape)


def solution(mesh):
    in_specs = (
        P(None, "gx", "gy", None),
        P("gx", "gy", None),
        P(None, "gx", "gy", None, None),
        P(None, "gx", "gy", None, None),
        P(None, "gx", "gy", None, None),
        P("gx", "gy", None),
        P("gx", "gy", None),
        P(),
    )
    out_specs = (P(None, "gx", "gy", None), P(None, "gx", "gy", None, None))
    return jax.shard_map(
        functools.partial(local, mesh), mesh=mesh, in_specs=in_specs, out_specs=out_specs,
        check_vma=False,
    )
```

profile of v0, /device:TPU:1, one launch (start us, length us, event | category | flops | bytes accessed | tf_op | source)
XLA Modules:
  0.0 45.2 jit_solution(5829549743429516956)
XLA Ops:
  0.6 42.3 %shard_map.95 = (f32[19,4,8,128]{3,2,1,0:T(8,128)}, f32[3,2,768]{2,1,0:T(2,128)}) custom-call(f32[19,4,8,128]{3,2,1,0:T(8,128)} %pops_ref.1, s32[4,8,128]{2,1,0:T(8,128)} %solid_ref.1, s32[3,2,768]{2,1,0:T(2,128)} %bitcast.10, f32[3,2,768]{2,1,0:T(2,128)} %bitcast.11, f32[3,2,768]{2,1,0:T(2,128)} %bitcast.12, f32[2]{0:T(128)} %bitcast.14, s32[2]{0:T(128)} %bitcast.15, ...), custom_call_target="tpu_custom_call" | custom-call | tf_op jit(solution)/shard_map/pallas_call | solution.py:497
  42.9 0.0 copy-start
  42.9 1.7 %copy.13 = f32[19,4,8,128]{3,2,1,0:T(8,128)} copy(f32[19,4,8,128]{3,2,1,0:T(8,128)} %get-tuple-element.10) | data formatting | bytes 622592
  44.6 0.0 copy-done
  44.6 0.6 %copy.14 = f32[3,1,1,2,768]{4,3,2,1,0:T(2,128)} copy(f32[3,1,1,2,768]{4,3,2,1,0:T(2,128)S(1)} %bitcast.13) | data formatting | bytes 36864
Async XLA Ops:
  42.9 1.7 %copy-start = (f32[3,2,768]{2,1,0:T(2,128)S(1)}, f32[3,2,768]{2,1,0:T(2,128)}, u32[]{:S(2)}) copy-start(f32[3,2,768]{2,1,0:T(2,128)} %get-tuple-element.5) | copy-start | bytes 55300
where the time goes:
time: 45.4 us; the launch traced here: 45.2 us
  Pallas kernels  42.3 us (93%)
  local copies, waits for them, and re-layouts  2.32 us (5%)
  between operations  0.65 us (1%)
    pallas_call x1, Pallas kernels, local(): pl.pallas_call(functools.partial(body_kernel, mesh.shape['gx'], mesh.shap...  42.3 us
    unnamed x4, local copies, waits for them, and re-layouts  2.32 us

commit v1 on v0

--- a/solution.py
+++ b/solution.py
@@ -152,52 +152,68 @@
 
 def body_kernel(
     peers_x, peers_y,
-    pops_ref, solid_ref, base_ref, offset_ref, rest_ref, stiff_ref, occ_ref, tri_ref,
+    pops_hbm, solid_hbm, base_hbm, offset_hbm, rest_hbm, stiff_hbm, occ_hbm, tri_hbm,
     pops_out, offset_out,
-    lap, off, spread, moved_ref, wide,
+    solid_ref, base_ref, offset_ref, rest_ref, stiff_ref, occ_ref, tri_ref,
+    incidence, lap, off, spread, moved_ref, wide,
     *scratch,
 ):
     recv_force, recv_pops, recv_mom = scratch[0:8], scratch[8:16], scratch[16:24]
     send_force, send_pops, send_mom = scratch[24:32], scratch[32:40], scratch[40:48]
     send_px, send_py, send_pc = send_pops[0:2], send_pops[2:4], send_pops[4:8]
     send_sem, recv_sem, load_sem = scratch[48:51]
-    rows_x = pops_ref.shape[1]
-    depth = pops_ref.shape[3]
+    rows_x = pops_out.shape[1]
+    depth = pops_out.shape[3]
     slots, padded = base_ref.shape[1], base_ref.shape[2]
     vertices = slots * padded
     planes = rows_x + 3
     ix, iy = lax.axis_index("gx"), lax.axis_index("gy")
     peer = [((ix + sx + peers_x) % peers_x, (iy + sy + peers_y) % peers_y) for sx, sy in DIRS]
 
-    load_pops = pltpu.make_async_copy(pops_ref, pops_out, load_sem)
-    load_pops.start()
+    loads = [
+        pltpu.make_async_copy(src, dst, load_sem.at[k])
+        for k, (src, dst) in enumerate((
+            (tri_hbm, tri_ref), (offset_hbm, offset_ref), (rest_hbm, rest_ref),
+            (base_hbm, base_ref), (stiff_hbm, stiff_ref), (occ_hbm, occ_ref),
+            (solid_hbm, solid_ref), (pops_hbm, pops_out),
+        ))
+    ]
+    for x in loads:
+        x.start()
     barrier = pltpu.get_barrier_semaphore()
     for p in peer:
         pl.semaphore_signal(barrier, inc=1, device_id=p, device_id_type=MESH)
 
+    loads[0].wait()
     faces = tri_ref.shape[1]
-    pairs = None
     for start in range(0, faces, 256):
         stop = min(start + 256, faces)
-        ids = lax.broadcasted_iota(jnp.int32, (base_ref.shape[2], stop - start), 0)
+        ids = lax.broadcasted_iota(jnp.int32, (padded, stop - start), 0)
         corner = [tri_ref[k : k + 1, start:stop] for k in range(3)]
         hit = (ids == corner[0]) | (ids == corner[1]) | (ids == corner[2])
-        part = jnp.where(hit, 1.0, 0.0).astype(jnp.bfloat16)
-        part = mm(part, part, NT)
-        pairs = part if pairs is None else pairs + part
-    same = lax.broadcasted_iota(jnp.int32, pairs.shape, 0) == lax.broadcasted_iota(
-        jnp.int32, pairs.shape, 1
-    )
-    lap_high, lap_low = split(jnp.where(same, -2.0 * pairs, pairs))
-    lap[0] = lap_high
-    lap[1] = lap_low
+        incidence[:, start:stop] = jnp.where(hit, 1.0, 0.0).astype(jnp.bfloat16)
+    for x in loads[1:6]:
+        x.wait()
+
+    def build_laplacian():
+        pairs = None
+        for start in range(0, faces, 256):
+            part = incidence[:, start : min(start + 256, faces)]
+            part = mm(part, part, NT)
+            pairs = part if pairs is None else pairs + part
+        same = lax.broadcasted_iota(jnp.int32, pairs.shape, 0) == lax.broadcasted_iota(
+            jnp.int32, pairs.shape, 1
+        )
+        lap_high, lap_low = split(jnp.where(same, -2.0 * pairs, pairs))
+        lap[0] = lap_high
+        lap[1] = lap_low
 
     def flat(ref):
         return jnp.concatenate([ref[:, m, :] for m in range(slots)], axis=1)
 
     base = flat(base_ref)
     base_x = base[0:1] - ix * rows_x
-    base_y = base[1:2] - iy * pops_ref.shape[2]
+    base_y = base[1:2] - iy * pops_out.shape[2]
     base_z = base[2:3]
     live = jnp.concatenate(
         [jnp.full((1, padded), occ_ref[m].astype(jnp.float32)) for m in range(slots)], axis=1
@@ -207,7 +223,6 @@
     )
     off[...] = flat(offset_ref)
     sub = lax.broadcasted_iota(jnp.int32, (8, depth), 0)
-    load_pops.wait()
 
     def copy(step, stage, d, src, dst):
         return pltpu.make_async_remote_copy(
@@ -257,16 +272,30 @@
                     value = jnp.concatenate([value[1:], side[None]], axis=0)
             pops_out[q] = value
 
-    def substep(step, carry):
+    def stacked(value):
+        high = value.astype(jnp.bfloat16).astype(jnp.float32)
+        return jnp.concatenate([high, value - high], axis=0).astype(jnp.bfloat16)
+
+    def substep(step, carry, first=False):
         now = off[...]
         strain = now - flat(rest_ref)
         six = jnp.concatenate(
             [strain[:, m * padded : (m + 1) * padded] for m in range(slots)], axis=0
         )
-        six_high = six.astype(jnp.bfloat16).astype(jnp.float32)
-        both = jnp.concatenate([six_high, six - six_high], axis=0).astype(jnp.bfloat16)
-        pulled = mm(both, lap[0], NN) + mm(both, lap[1], NN)
-        pulled = pulled[0 : 3 * slots] + pulled[3 * slots :]
+        if first:
+            summed = mm(stacked(six), incidence[...], NN)
+            summed = summed[0 : 3 * slots] + summed[3 * slots :]
+            both = jnp.concatenate(
+                [stacked(summed), jnp.ones((1, faces), jnp.bfloat16)], axis=0
+            )
+            pulled = mm(both, incidence[...], NT)
+            count = pulled[6 * slots :]
+            pulled = pulled[0 : 3 * slots] + pulled[3 * slots : 6 * slots]
+            pulled = pulled - 3.0 * count * six
+        else:
+            both = stacked(six)
+            pulled = mm(both, lap[0], NN) + mm(both, lap[1], NN)
+            pulled = pulled[0 : 3 * slots] + pulled[3 * slots :]
         force_v = scale * jnp.concatenate(
             [pulled[3 * m : 3 * m + 3] for m in range(slots)], axis=1
         )
@@ -309,15 +338,16 @@
                 tiles = pack(tiles, 0 if sy == 1 else 7, 2 if sy == 1 else 1)
             for k, tile in enumerate(tiles):
                 send_force[d][step, k] = tile
-        @pl.when(step == 0)
-        def _():
+        if first:
             pl.semaphore_wait(barrier, len(peer))
-
         launch(step, 0)
         spread_tiles([(x, a, 0) for x in range(rows_x) for a in range(3)], 8 * len(outer))
 
-        @pl.when(step > 0)
-        def _():
+        if first:
+            build_laplacian()
+            loads[6].wait()
+            loads[7].wait()
+        else:
             finish_pops(step - 1)
 
         arrive(step, 0)
@@ -455,7 +485,8 @@
         off[...] = now + live * jnp.concatenate(drift, axis=0)
         return carry
 
-    lax.fori_loop(0, SUBSTEPS, substep, 0)
+    substep(0, 0, True)
+    lax.fori_loop(1, SUBSTEPS, substep, 0)
     finish_pops(SUBSTEPS - 1)
 
     for m in range(slots):
@@ -468,6 +499,17 @@
         return carry
 
     lax.fori_loop(0, SUBSTEPS, drain, 0)
+
+
+def write_kernel(pops_ref, offset_ref, pops_out, offset_out, sem):
+    copies = [
+        pltpu.make_async_copy(pops_ref, pops_out, sem.at[0]),
+        pltpu.make_async_copy(offset_ref, offset_out, sem.at[1]),
+    ]
+    for x in copies:
+        x.start()
+    for x in copies:
+        x.wait()
 
 
 def local(mesh, populations, solid, base_cell, offset, rest, stiffness, occupied, triangles):
@@ -480,7 +522,12 @@
     tile = (8, depth)
     pop_shapes = [(5,)] * 2 + [(rows_x,)] * 2 + [()] * 4
     V = lambda shape, dtype=f32: pltpu.VMEM(shape, dtype)
+    small = (3, slots, padded)
+    i32 = jnp.int32
     scratch = [
+        V(solid.shape, i32), V(small, i32), V(small), V(small),
+        pltpu.SMEM((slots,), f32), pltpu.SMEM((slots,), i32), V(triangles.shape[::-1], i32),
+        V((padded, triangles.shape[0]), bf16),
         V((2, padded, padded), bf16), V((3, vertices)),
         V((2, planes * 48, vertices), bf16),
         V((19, rows_x) + tile), V((planes, 3, 2) + tile),
@@ -490,26 +537,35 @@
         scratch += [V((S,) + p + tile) for p in pop_shapes]
         scratch += [V((S, moment_size(*d, rows_x)) + tile) for d in DIRS]
     scratch += [pltpu.SemaphoreType.DMA((S, 3, 8)), pltpu.SemaphoreType.DMA((S, 3, 8))]
-    scratch += [pltpu.SemaphoreType.DMA(())]
+    scratch += [pltpu.SemaphoreType.DMA((8,))]
     vmem = pl.BlockSpec(memory_space=pltpu.VMEM)
-    smem = pl.BlockSpec(memory_space=pltpu.SMEM)
-    small = (3, slots, padded)
+    hbm = pl.BlockSpec(memory_space=pltpu.HBM)
     pops, moved = pl.pallas_call(
         functools.partial(body_kernel, mesh.shape["gx"], mesh.shape["gy"]),
-        out_shape=(
-            jax.ShapeDtypeStruct(populations.shape, f32),
-            jax.ShapeDtypeStruct(small, f32),
-        ),
-        in_specs=[pl.BlockSpec(memory_space=pl.ANY)] + [vmem] * 4 + [smem] * 2 + [vmem],
+        out_shape=(pltpu.VMEM(populations.shape, f32), pltpu.VMEM(small, f32)),
+        in_specs=[hbm] * 8,
         out_specs=(vmem, vmem),
         scratch_shapes=scratch,
         compiler_params=pltpu.CompilerParams(
-            collective_id=0, has_side_effects=True, vmem_limit_bytes=60 * 1024 * 1024
+            collective_id=0, has_side_effects=True, vmem_limit_bytes=24 * 1024 * 1024
         ),
-    )(
-        populations, solid, base_cell.reshape(small), offset.reshape(small), rest.reshape(small),
-        stiffness.reshape(slots), occupied.reshape(slots), triangles.T,
-    )
+    )(*[
+        pltpu.with_memory_space_constraint(x, pltpu.HBM)
+        for x in (
+            populations, solid, base_cell.reshape(small), offset.reshape(small),
+            rest.reshape(small), stiffness.reshape(slots), occupied.reshape(slots), triangles.T,
+        )
+    ])
+    pops, moved = pl.pallas_call(
+        write_kernel,
+        out_shape=(
+            jax.ShapeDtypeStruct(populations.shape, f32), jax.ShapeDtypeStruct(small, f32),
+        ),
+        in_specs=[pl.BlockSpec(memory_space=pl.ANY)] * 2,
+        out_specs=(hbm, hbm),
+        scratch_shapes=[pltpu.SemaphoreType.DMA((2,))],
+        compiler_params=pltpu.CompilerParams(vmem_limit_bytes=1024 * 1024),
+    )(pops, moved)
     return pops, moved.reshape(offset.shape)
 
 

time: 45.4 us -> 42.2 us (0.930)
  local copies, waits for them, and re-layouts: 2.32 us -> 0 us
  Pallas kernels: 42.3 us -> 41.4 us
    unnamed x4 -> x0, local copies, waits for them, and re-layouts: 2.32 us -> none
    pallas_call x1, Pallas kernels: 42.3 us -> 40.7 us  [local(): pl.pallas_call(functools.partial(body_kernel, mesh.shape['gx'], mesh.shap...]
    pallas_call x0 -> x1, Pallas kernels: none -> 0.74 us  [local(): pl.pallas_call(write_kernel, out_shape=(jax.ShapeDtypeStruct(populations....]
where the time goes in v1:
time: 42.2 us; the launch traced here: 42.1 us
  Pallas kernels  41.4 us (98%)
  between operations  0.64 us (2%)
    pallas_call x1, Pallas kernels, local(): pl.pallas_call(functools.partial(body_kernel, mesh.shape['gx'], mesh.shap...  40.7 us

profile of v1, /device:TPU:1, one launch (start us, length us, event | category | flops | bytes accessed | tf_op | source)
XLA Modules:
  0.0 42.1 jit_solution(2862605089868868539)
XLA Ops:
  0.6 40.7 %shard_map.95 = (f32[19,4,8,128]{3,2,1,0:T(8,128)S(1)}, f32[3,2,768]{2,1,0:T(2,128)S(1)}) custom-call(f32[19,4,8,128]{3,2,1,0:T(8,128)} %pops_hbm.1, s32[4,8,128]{2,1,0:T(8,128)} %solid_hbm.1, s32[3,2,768]{2,1,0:T(2,128)} %bitcast.10, f32[3,2,768]{2,1,0:T(2,128)} %bitcast.11, f32[3,2,768]{2,1,0:T(2,128)} %bitcast.12, f32[2]{0:T(128)} %bitcast.13, ...), custom_call_target="tpu_custom_call" | custom-call | tf_op jit(solution)/shard_map/pallas_call | solution.py:543
  41.3 0.7 %shard_map.96 = (f32[19,4,8,128]{3,2,1,0:T(8,128)}, f32[3,2,768]{2,1,0:T(2,128)}) custom-call(f32[19,4,8,128]{3,2,1,0:T(8,128)S(1)} %get-tuple-element.6.pops_ref, f32[3,2,768]{2,1,0:T(2,128)S(1)} %get-tuple-element.7.offset_ref), custom_call_target="tpu_custom_call" | custom-call | tf_op jit(solution)/shard_map/pallas_call | solution.py:559

commit v2 on v1

--- a/solution.py
+++ b/solution.py
@@ -17,6 +17,7 @@
 OPPOSITE = [0, 2, 1, 4, 3, 6, 5, 8, 7, 10, 9, 12, 11, 14, 13, 16, 15, 18, 17]
 LATTICE_WEIGHTS = [1.0 / 3.0] + [1.0 / 18.0] * 6 + [1.0 / 36.0] * 12
 RELAX = 0.8
+CHUNK = 256
 XS = {s: [q for q in range(19) if VELOCITIES[q][0] == s] for s in (1, -1)}
 YS = {s: [q for q in range(19) if VELOCITIES[q][1] == s] for s in (1, -1)}
 CORNER = {(v[0], v[1]): q for q, v in enumerate(VELOCITIES) if v[0] and v[1]}
@@ -38,7 +39,7 @@
 
 def quarter_sine(t):
     t = t - 4.0 * jnp.floor(t * 0.25 + 0.5)
-    t = jnp.where(t > 1.0, 2.0 - t, jnp.where(t < -1.0, -2.0 - t, t))
+    t = jnp.maximum(jnp.minimum(t, 2.0 - t), -2.0 - t)
     x = t * (math.pi / 2.0)
     u = x * x
     p = 1.0 / 6227020800.0
@@ -47,13 +48,9 @@
     return x * p
 
 
-def table(rows, base, kernels):
+def distance(rows, base):
     cells = lax.broadcasted_iota(jnp.int32, (rows, base.shape[1]), 0)
-    d = (cells - base + 1) & (rows - 1)
-    out = jnp.where(d == 3, kernels[3], 0.0)
-    for s in (2, 1, 0):
-        out = jnp.where(d == s, kernels[s], out)
-    return out
+    return (cells - base + 1) & (rows - 1)
 
 
 def moments(pops):
@@ -69,28 +66,46 @@
     return density, momentum
 
 
-def collide(pops, force, walled):
+def settle(pops, walled):
     density, momentum = moments(pops)
+    kept = 1.0 - 1.0 / RELAX
+    still = [jnp.where(walled, pops[OPPOSITE[q]], kept * pops[q]) for q in range(19)]
+    return density, momentum, still
+
+
+def collide(density, momentum, still, force, walled):
     inverse = 1.0 / density
-    u = [(momentum[a] + 0.5 * force[a]) * inverse for a in range(3)]
-    squared = u[0] * u[0] + u[1] * u[1] + u[2] * u[2]
+    rate, keep = 1.0 / RELAX, 1.0 - 0.5 / RELAX
+    n = [momentum[a] + 0.5 * force[a] for a in range(3)]
+    u = [jnp.where(walled, 0.0, n[a] * inverse) for a in range(3)]
+    squared = u[0] * n[0] + u[1] * n[1] + u[2] * n[2]
     working = u[0] * force[0] + u[1] * force[1] + u[2] * force[2]
-    base = 1.0 - 1.5 * squared
-    relaxed = []
-    for q in range(19):
+    even = rate * density - (1.5 * rate) * squared - (3.0 * keep) * working
+    w = LATTICE_WEIGHTS[1]
+    odd = [(3.0 * rate * w) * n[a] + (3.0 * keep * w) * force[a] for a in range(3)]
+    twice = [(4.5 * rate * w) * n[a] + (9.0 * keep * w) * force[a] for a in range(3)]
+    even = jnp.where(walled, 0.0, even)
+    odd = [jnp.where(walled, 0.0, x) for x in odd]
+    axis_even, half_even = w * even, (0.5 * w) * even
+    half_odd, half_twice = [0.5 * x for x in odd], [0.5 * x for x in twice]
+
+    def dot(vector, values):
+        terms = [(vector[a], values[a]) for a in range(3) if vector[a]]
+        out = terms[0][1] if terms[0][0] == 1 else -terms[0][1]
+        for sign, value in terms[1:]:
+            out = out + value if sign == 1 else out - value
+        return out
+
+    fresh = {0: LATTICE_WEIGHTS[0] * even}
+    for q in range(1, 19, 2):
         vector = VELOCITIES[q]
-        along, pushed = jnp.zeros_like(density), jnp.zeros_like(density)
-        for a in range(3):
-            if vector[a] == 1:
-                along, pushed = along + u[a], pushed + force[a]
-            elif vector[a] == -1:
-                along, pushed = along - u[a], pushed - force[a]
-        w = LATTICE_WEIGHTS[q]
-        equilibrium = (w * density) * (base + along * (3.0 + 4.5 * along))
-        source = ((1.0 - 0.5 / RELAX) * w) * (3.0 * (pushed - working) + 9.0 * along * pushed)
-        updated = pops[q] - (pops[q] - equilibrium) * (1.0 / RELAX) + source
-        relaxed.append(jnp.where(walled, pops[OPPOSITE[q]], updated))
-    return relaxed
+        diagonal = sum(abs(v) for v in vector) == 2
+        push = dot(vector, half_odd if diagonal else odd)
+        mid = (half_even if diagonal else axis_even) + dot(vector, u) * dot(
+            vector, half_twice if diagonal else twice
+        )
+        fresh[q], fresh[OPPOSITE[q]] = mid + push, mid - push
+    return [still[q] + fresh[q] for q in range(19)]
 
 
 def roll(x, shift, axis):
@@ -138,12 +153,20 @@
 
 def force_size(sx, sy, rows_x):
     n = 3 * len(force_planes(sx, rows_x))
-    return {0: n, 1: packed(n, 2), -1: packed(n, 1)}[sy]
+    return n if sy == 0 else -(-n * (2 if sy == 1 else 1) // 8)
 
 
 def moment_size(sx, sy, rows_x):
     n = 4 * len(moment_planes(sx, rows_x))
     return {0: n + packed(n, 2), 1: packed(n, 2), -1: packed(n, 1) + packed(n, 2)}[sy]
+
+
+def stage_sizes(rows_x, stage):
+    force = [force_size(*d, rows_x) for d in DIRS]
+    moment = [moment_size(*d, rows_x) for d in DIRS]
+    pops = [len(XS[1])] * 2 + [rows_x] * 2 + [1] * 4
+    sizes = (force, moment, pops)
+    return sum(sum(x) for x in sizes[:stage]), sizes[stage]
 
 
 def total_of(parts):
@@ -155,18 +178,14 @@
     pops_hbm, solid_hbm, base_hbm, offset_hbm, rest_hbm, stiff_hbm, occ_hbm, tri_hbm,
     pops_out, offset_out,
     solid_ref, base_ref, offset_ref, rest_ref, stiff_ref, occ_ref, tri_ref,
-    incidence, lap, off, spread, moved_ref, wide,
-    *scratch,
+    incidence, lap, off, spread, deep, masks, masks_z, moved_ref, wide,
+    send_buf, recv_buf, send_sem, recv_sem, load_sem,
 ):
-    recv_force, recv_pops, recv_mom = scratch[0:8], scratch[8:16], scratch[16:24]
-    send_force, send_pops, send_mom = scratch[24:32], scratch[32:40], scratch[40:48]
-    send_px, send_py, send_pc = send_pops[0:2], send_pops[2:4], send_pops[4:8]
-    send_sem, recv_sem, load_sem = scratch[48:51]
     rows_x = pops_out.shape[1]
     depth = pops_out.shape[3]
     slots, padded = base_ref.shape[1], base_ref.shape[2]
     vertices = slots * padded
-    planes = rows_x + 3
+    chunks = [slice(k, min(k + CHUNK, vertices)) for k in range(0, vertices, CHUNK)]
     ix, iy = lax.axis_index("gx"), lax.axis_index("gy")
     peer = [((ix + sx + peers_x) % peers_x, (iy + sy + peers_y) % peers_y) for sx, sy in DIRS]
 
@@ -184,29 +203,22 @@
     for p in peer:
         pl.semaphore_signal(barrier, inc=1, device_id=p, device_id_type=MESH)
 
-    loads[0].wait()
+    for x in loads[:6]:
+        x.wait()
     faces = tri_ref.shape[1]
-    for start in range(0, faces, 256):
-        stop = min(start + 256, faces)
-        ids = lax.broadcasted_iota(jnp.int32, (padded, stop - start), 0)
-        corner = [tri_ref[k : k + 1, start:stop] for k in range(3)]
-        hit = (ids == corner[0]) | (ids == corner[1]) | (ids == corner[2])
-        incidence[:, start:stop] = jnp.where(hit, 1.0, 0.0).astype(jnp.bfloat16)
-    for x in loads[1:6]:
-        x.wait()
+    parts = [slice(k, min(k + 256, faces)) for k in range(0, faces, 256)]
 
     def build_laplacian():
         pairs = None
-        for start in range(0, faces, 256):
-            part = incidence[:, start : min(start + 256, faces)]
-            part = mm(part, part, NT)
+        for cut in parts:
+            part = mm(incidence[:, cut], incidence[:, cut], NT)
             pairs = part if pairs is None else pairs + part
         same = lax.broadcasted_iota(jnp.int32, pairs.shape, 0) == lax.broadcasted_iota(
             jnp.int32, pairs.shape, 1
         )
         lap_high, lap_low = split(jnp.where(same, -2.0 * pairs, pairs))
-        lap[0] = lap_high
-        lap[1] = lap_low
+        lap[:, 0:padded] = lap_high
+        lap[:, padded:] = lap_low
 
     def flat(ref):
         return jnp.concatenate([ref[:, m, :] for m in range(slots)], axis=1)
@@ -221,23 +233,50 @@
     scale = live * jnp.concatenate(
         [jnp.full((1, padded), stiff_ref[m]) for m in range(slots)], axis=1
     )
+    lane = lax.broadcasted_iota(jnp.int32, scale.shape, 1)
+    scale = jnp.where((lane // CHUNK) % 2 == 1, -scale, scale)
     off[...] = flat(offset_ref)
     sub = lax.broadcasted_iota(jnp.int32, (8, depth), 0)
-
-    def copy(step, stage, d, src, dst):
+    distances = ((8, base_x, 0), (16, base_y, 8), (depth, base_z, 24))
+
+    for rows, base_row, start in distances:
+        d = distance(rows, base_row)
+        fits = [
+            jnp.where(d < 4, 0.25, 0.0),
+            jnp.where(d == 1, 1.0, jnp.where(d == 3, -1.0, 0.0)),
+            jnp.where(d == 2, 1.0, jnp.where(d == 0, -1.0, 0.0)),
+        ]
+        for k in range(3):
+            if rows == depth:
+                masks_z[k] = fits[k].astype(jnp.bfloat16)
+            else:
+                masks[k, start : start + rows, :] = fits[k]
+
+    def place(stage, d):
+        start = stage_sizes(rows_x, stage)[0]
+        sizes = stage_sizes(rows_x, stage)[1]
+        return start + sum(sizes[:d]), sizes[d]
+
+    def copy(step, stage, start, size, device):
+        part = pl.ds(start, size)
         return pltpu.make_async_remote_copy(
-            src_ref=src, dst_ref=dst.at[step], send_sem=send_sem.at[step, stage, d],
-            recv_sem=recv_sem.at[step, stage, d], device_id=peer[d], device_id_type=MESH,
-        )
-
-    groups = ((send_force, recv_force), (send_mom, recv_mom), (send_pops, recv_pops))
-
-    def copies(step, stage):
-        src, dst = groups[stage]
-        return [copy(step, stage, d, src[d].at[step], dst[d]) for d in range(8)]
+            src_ref=send_buf.at[step, part], dst_ref=recv_buf.at[step, part],
+            send_sem=send_sem.at[step, stage], recv_sem=recv_sem.at[step, stage],
+            device_id=device, device_id_type=MESH,
+        )
+
+    def whole(step, stage):
+        start, sizes = stage_sizes(rows_x, stage)
+        return copy(step, stage, start, sum(sizes), peer[0])
+
+    def put(step, stage, d, k, tile):
+        send_buf[step, place(stage, d)[0] + k] = tile
+
+    def got(step, stage, d, k):
+        return recv_buf[step, place(stage, d)[0] + k]
 
     def launch(step, stage):
-        sends = copies(step, stage)
+        sends = [copy(step, stage, *place(stage, d), peer[d]) for d in range(8)]
 
         @pl.when(iy % 2 == 1)
         def _():
@@ -250,12 +289,13 @@
                 sends[d].start()
 
     def arrive(step, stage):
-        for x in copies(step, stage):
-            x.wait_recv()
+        whole(step, stage).wait_recv()
 
     def finish_pops(step):
         arrive(step, 2)
-        from_y = {1: recv_pops[2][step], -1: recv_pops[3][step]}
+        from_y = {
+            sy: jnp.stack([got(step, 2, d, x) for x in range(rows_x)]) for d, sy in ((2, 1), (3, -1))
+        }
         for q in range(19):
             sx, sy, _ = VELOCITIES[q]
             value = moved_ref[q]
@@ -263,9 +303,9 @@
             if sy:
                 value = jnp.where(edge_row, roll(from_y[sy], -YS[sy].index(q), 1), value)
             if sx:
-                side = recv_pops[0 if sx == 1 else 1][step, XS[sx].index(q)]
+                side = got(step, 2, 0 if sx == 1 else 1, XS[sx].index(q))
                 if sy:
-                    side = jnp.where(edge_row, recv_pops[DIRS.index((sx, sy))][step], side)
+                    side = jnp.where(edge_row, got(step, 2, DIRS.index((sx, sy)), 0), side)
                 if sx == 1:
                     value = jnp.concatenate([side[None], value[:-1]], axis=0)
                 else:
@@ -278,70 +318,95 @@
 
     def substep(step, carry, first=False):
         now = off[...]
+        waves = quarter_sine(jnp.concatenate([now, now + 1.0], axis=0)) * 0.25
+        table_x, table_y = [
+            masks[0, start : start + rows, :]
+            + waves[3 + k : 4 + k] * masks[1, start : start + rows, :]
+            + waves[k : k + 1] * masks[2, start : start + rows, :]
+            for k, (rows, _, start) in enumerate(distances[:2])
+        ]
+        coarse = jnp.floor(waves * 512.0 + 0.5) * (1.0 / 512.0)
+        fine = waves - coarse
+        sine, cosine, sine_low, cosine_low = [
+            jnp.broadcast_to(x, (depth, vertices)).astype(jnp.bfloat16)
+            for x in (coarse[2:3], coarse[5:6], fine[2:3], fine[5:6])
+        ]
+        deep[0:depth, :] = masks_z[0] + cosine * masks_z[1] + sine * masks_z[2]
+        deep[depth:, :] = cosine_low * masks_z[1] + sine_low * masks_z[2]
         strain = now - flat(rest_ref)
         six = jnp.concatenate(
             [strain[:, m * padded : (m + 1) * padded] for m in range(slots)], axis=0
         )
         if first:
-            summed = mm(stacked(six), incidence[...], NN)
-            summed = summed[0 : 3 * slots] + summed[3 * slots :]
-            both = jnp.concatenate(
-                [stacked(summed), jnp.ones((1, faces), jnp.bfloat16)], axis=0
-            )
-            pulled = mm(both, incidence[...], NT)
+            pulled, pair = None, stacked(six)
+            for cut in parts:
+                shape = (padded, cut.stop - cut.start)
+                ids = lax.broadcasted_iota(jnp.int32, shape, 0).astype(jnp.int16)
+                hit = None
+                for k in range(3):
+                    corner = jnp.broadcast_to(tri_ref[k : k + 1, cut], shape).astype(jnp.int16)
+                    hit = ids == corner if hit is None else hit | (ids == corner)
+                one = jnp.ones(shape, jnp.bfloat16)
+                incidence[:, cut] = jnp.where(hit, one, jnp.zeros(shape, jnp.bfloat16))
+                summed = mm(pair, incidence[:, cut], NN)
+                summed = summed[0 : 3 * slots] + summed[3 * slots :]
+                ones = jnp.ones((1, summed.shape[1]), jnp.bfloat16)
+                part = mm(
+                    jnp.concatenate([stacked(summed), ones], axis=0), incidence[:, cut], NT
+                )
+                pulled = part if pulled is None else pulled + part
             count = pulled[6 * slots :]
             pulled = pulled[0 : 3 * slots] + pulled[3 * slots : 6 * slots]
             pulled = pulled - 3.0 * count * six
         else:
-            both = stacked(six)
-            pulled = mm(both, lap[0], NN) + mm(both, lap[1], NN)
+            pulled = mm(stacked(six), lap[...], NN)
+            pulled = pulled[:, 0:padded] + pulled[:, padded:]
             pulled = pulled[0 : 3 * slots] + pulled[3 * slots :]
         force_v = scale * jnp.concatenate(
             [pulled[3 * m : 3 * m + 3] for m in range(slots)], axis=1
         )
-        s = quarter_sine(now) * 0.25
-        c = quarter_sine(now + 1.0) * 0.25
-        kernels = (0.25 - s, 0.25 + c, 0.25 + s, 0.25 - c)
-        table_x = table(8, base_x, [k[0:1] for k in kernels])
-        table_y = table(16, base_y, [k[1:2] for k in kernels])
-        deep_high, deep_low = split(table(depth, base_z, [k[2:3] for k in kernels]))
-        deep = jnp.concatenate([deep_high, deep_low], axis=0)
+        pulled_x = [force_v[a : a + 1] * table_x for a in range(3)]
         tiles_of = {}
 
         def spread_tiles(names, start):
-            for n in range(0, len(names), 2):
-                blocks = [
-                    (force_v[a : a + 1] * table_x[x & 7 : (x & 7) + 1])
-                    * table_y[8 * t : 8 * t + 8]
-                    for x, a, t in names[n : n + 2]
-                ]
-                high, low = split(jnp.concatenate(blocks, axis=0))
-                row = start + 8 * n
-                spread[0, row : row + 16, :] = high
-                spread[1, row : row + 16, :] = low
-            stop = start + 8 * len(names)
-            first = mm(spread[0, start:stop], deep, NT)
-            total = first[:, :depth] + first[:, depth:]
-            total = total + mm(spread[1, start:stop], deep_high, NT)
+            half, sums = 8 * len(names), [None, None]
+            for c, cut in enumerate(chunks):
+                for n in range(0, len(names), 2):
+                    blocks = [
+                        pulled_x[a][:, cut] * table_y[y : y + 1, cut] if x is None
+                        else pulled_x[a][x & 7 : (x & 7) + 1, cut] * table_y[0:8, cut]
+                        for x, a, y in names[n : n + 2]
+                    ]
+                    high, low = split(jnp.concatenate(blocks, axis=0))
+                    row = start + 8 * n
+                    spread[row : row + 16, cut] = high
+                    spread[row + half : row + half + 16, cut] = low
+                part = mm(spread[start : start + 2 * half, cut], deep[:, cut], NT)
+                sums[c % 2] = part if sums[c % 2] is None else sums[c % 2] + part
+            total = sums[0] - sums[1]
+            total = total[:half, :depth] + total[:half, depth:] + total[half:, :depth]
             for n, name in enumerate(names):
                 tiles_of[name] = total[8 * n : 8 * n + 8]
 
-        outer = [(x, a, t) for x in (rows_x, rows_x + 1, -1) for a in range(3) for t in (0, 1)]
-        outer += [(x, a, 1) for x in range(rows_x) for a in range(3)]
+        far_y = (8, 9, 15)
+        outer = [(None, a, y) for y in far_y for a in range(3)]
+        outer += [(x, a, 0) for x in (rows_x, rows_x + 1, -1) for a in range(3)]
         spread_tiles(outer, 0)
         for d, (sx, sy) in enumerate(DIRS):
-            tiles = [
-                tiles_of[x, a, 0 if sy == 0 else 1]
-                for x in force_planes(sx, rows_x) for a in range(3)
-            ]
-            if sy:
-                tiles = pack(tiles, 0 if sy == 1 else 7, 2 if sy == 1 else 1)
+            across = force_planes(sx, rows_x)
+            if sy == 0:
+                tiles = [tiles_of[x, a, 0] for x in across for a in range(3)]
+            else:
+                tiles = [
+                    tiles_of[None, a, y] for y in ((8, 9) if sy == 1 else (15,)) for a in range(3)
+                ]
+                tiles = pack(tiles, across[0] & 7, len(across))
             for k, tile in enumerate(tiles):
-                send_force[d][step, k] = tile
+                put(step, 0, d, k, tile)
         if first:
             pl.semaphore_wait(barrier, len(peer))
         launch(step, 0)
-        spread_tiles([(x, a, 0) for x in range(rows_x) for a in range(3)], 8 * len(outer))
+        spread_tiles([(x, a, 0) for x in range(rows_x) for a in range(3)], 16 * len(outer))
 
         if first:
             build_laplacian()
@@ -350,26 +415,41 @@
         else:
             finish_pops(step - 1)
 
+        walled = solid_ref[...] != 0
+        density, momentum, still = settle([pops_out[q] for q in range(19)], walled)
+        for q in range(19):
+            pops_out[q] = still[q]
         arrive(step, 0)
-        parts = {(x, a): [tiles_of[x, a, 0]] for x in range(rows_x) for a in range(3)}
+        force = [[tiles_of[x, a, 0] for x in range(rows_x)] for a in range(3)]
+        edge = {(y, a): None for y in (0, 1, 7) for a in range(3)}
         for d, (sx, sy) in enumerate(DIRS):
-            names = [
-                (landing(x, sx, rows_x), a) for x in force_planes(sx, rows_x) for a in range(3)
-            ]
-            load = lambda k, d=d: recv_force[d][step, k]
+            load = lambda k, d=d: got(step, 0, d, k)
+            planes_in = force_planes(sx, rows_x)
             if sy == 0:
-                tiles = [load(k) for k in range(len(names))]
-            else:
-                start, rows = (0, 2) if sy == 1 else (7, 1)
-                mask = row_mask(start, rows, depth)
-                tiles = [jnp.where(mask, t, 0.0) for t in unpack(load, len(names), rows)]
-            for name, tile in zip(names, tiles):
-                parts[name].append(tile)
-        force = [
-            jnp.stack([total_of(parts[x, a]) for x in range(rows_x)]) for a in range(3)
-        ]
-
-        relaxed = collide([pops_out[q] for q in range(19)], force, solid_ref[...] != 0)
+                for k, x in enumerate(planes_in):
+                    for a in range(3):
+                        here = force[a][landing(x, sx, rows_x)]
+                        force[a][landing(x, sx, rows_x)] = here + load(3 * k + a)
+                continue
+            names = [(y, a) for y in ((0, 1) if sy == 1 else (7,)) for a in range(3)]
+            rows, per = len(planes_in), 8 // len(planes_in)
+            sent, land = planes_in[0] & 7, landing(planes_in[0], sx, rows_x)
+            mask = row_mask(land, rows, depth)
+            for k, name in enumerate(names):
+                tile = roll(load(k // per), land - sent - (k % per) * rows, 0)
+                tile = jnp.where(mask, tile, 0.0)
+                edge[name] = tile if edge[name] is None else edge[name] + tile
+        for a in range(3):
+            for x in range(rows_x):
+                tile = jnp.where(sub == 0, roll(edge[0, a], -x, 0), 0.0)
+                for y in (1, 7):
+                    tile = jnp.where(sub == y, roll(edge[y, a], y - x, 0), tile)
+                force[a][x] = force[a][x] + tile
+        force = [jnp.stack(force[a]) for a in range(3)]
+
+        relaxed = collide(
+            density, momentum, [pops_out[q] for q in range(19)], force, walled
+        )
         moved = [
             roll(roll(relaxed[q], VELOCITIES[q][2], 2), VELOCITIES[q][1], 1) for q in range(19)
         ]
@@ -417,20 +497,21 @@
             else:
                 tiles = pack(far, 7, 1) + pack(near, 0, 2)
             for k, tile in enumerate(tiles):
-                send_mom[d][step, k] = tile
+                put(step, 1, d, k, tile)
         launch(step, 1)
         for n, sx in enumerate((1, -1)):
             edge = rows_x - 1 if sx == 1 else 0
             for k, q in enumerate(XS[sx]):
-                send_px[n][step, k] = moved[q][edge]
+                put(step, 2, n, k, moved[q][edge])
         for n, sy in enumerate((1, -1)):
             rows_kept = moved[YS[sy][0]]
             start = 0 if sy == 1 else 7
             for k, q in enumerate(YS[sy][1:], 1):
                 rows_kept = jnp.where(sub == (start + k) % 8, roll(moved[q], k, 1), rows_kept)
-            send_py[n][step] = rows_kept
+            for x in range(rows_x):
+                put(step, 2, 2 + n, x, rows_kept[x])
         for n, (sx, sy) in enumerate(DIRS[4:]):
-            send_pc[n][step] = moved[CORNER[sx, sy]][rows_x - 1 if sx == 1 else 0]
+            put(step, 2, 4 + n, 0, moved[CORNER[sx, sy]][rows_x - 1 if sx == 1 else 0])
         launch(step, 2)
         arrive(step, 1)
         reach = [x for x in range(rows_x + 2)] + [-1]
@@ -446,7 +527,7 @@
                 for x in moment_planes(sx, rows_x) for c in range(4)
             ]
             count = len(names)
-            load = lambda k, d=d: recv_mom[d][step, k]
+            load = lambda k, d=d: got(step, 1, d, k)
             if sy == 0:
                 a = [load(k) for k in range(count)]
                 b = unpack(lambda k: load(count + k), count, 2)
@@ -464,25 +545,40 @@
                 near[name].append(p)
                 far[name].append(r)
         used = row_mask(7, 3, depth)
+        count = len(reach)
         for i, x in enumerate(reach):
-            for t, side in enumerate((near, far)):
-                dens = total_of(side[x, 0])
-                if t:
-                    dens = jnp.where(used, dens, 1.0)
-                inverse = 1.0 / dens
-                for a in range(3):
-                    wide[i, a, t] = total_of(side[x, a + 1]) * inverse
-        wide_high, wide_low = split(wide[...].reshape(planes * 3 * 16, depth))
+            inverse = 1.0 / total_of(near[x, 0])
+            for a in range(3):
+                wide[a, i] = total_of(near[x, a + 1]) * inverse
+        speed = {}
+        for x in reach:
+            inverse = 1.0 / jnp.where(used, total_of(far[x, 0]), 1.0)
+            for a in range(3):
+                speed[x, a] = total_of(far[x, a + 1]) * inverse
+        for k, y in enumerate(far_y):
+            for a in range(3):
+                tile = jnp.zeros((8, depth), jnp.float32)
+                for x in reach:
+                    tile = jnp.where(sub == (x & 7), roll(speed[x, a], x - y, 0), tile)
+                wide[a, count + k] = tile
+        wide_high, wide_low = split(wide[...].reshape((count + 3) * 24, depth))
         twice = jnp.concatenate([wide_high, wide_high], axis=1)
-        along = mm(twice, deep, NN) + mm(wide_low, deep_high, NN)
-        along = along.reshape(planes, 3, 16, vertices)
-        drift, order = [], list(range(rows_x + 2)) + [7]
-        for a in range(3):
-            acc = along[0, a] * table_x[0:1]
-            for i, x in enumerate(order[1:], 1):
-                acc = acc + along[i, a] * table_x[x : x + 1]
-            drift.append(jnp.sum(acc * table_y, axis=0, keepdims=True))
-        off[...] = now + live * jnp.concatenate(drift, axis=0)
+        pieces = []
+        for cut in chunks:
+            along = mm(twice, deep[:, cut], NN) + mm(wide_low, deep[0:depth, cut], NN)
+            along = along.reshape(3, count + 3, 8, along.shape[1])
+            drift = []
+            for a in range(3):
+                near_sum = total_of([
+                    along[a, i] * table_x[x & 7 : (x & 7) + 1, cut] for i, x in enumerate(reach)
+                ])
+                far_sum = total_of([
+                    along[a, count + k] * table_y[y : y + 1, cut] for k, y in enumerate(far_y)
+                ])
+                total = near_sum * table_y[0:8, cut] + far_sum * table_x[:, cut]
+                drift.append(jnp.sum(total, axis=0, keepdims=True))
+            pieces.append(jnp.concatenate(drift, axis=0))
+        off[...] = now + live * jnp.concatenate(pieces, axis=1)
         return carry
 
     substep(0, 0, True)
@@ -494,8 +590,7 @@
 
     def drain(step, carry):
         for stage in range(3):
-            for x in copies(step, stage):
-                x.wait_send()
+            whole(step, stage).wait_send()
         return carry
 
     lax.fori_loop(0, SUBSTEPS, drain, 0)
@@ -520,7 +615,6 @@
     S = SUBSTEPS
     f32, bf16 = jnp.float32, jnp.bfloat16
     tile = (8, depth)
-    pop_shapes = [(5,)] * 2 + [(rows_x,)] * 2 + [()] * 4
     V = lambda shape, dtype=f32: pltpu.VMEM(shape, dtype)
     small = (3, slots, padded)
     i32 = jnp.int32
@@ -528,15 +622,14 @@
         V(solid.shape, i32), V(small, i32), V(small), V(small),
         pltpu.SMEM((slots,), f32), pltpu.SMEM((slots,), i32), V(triangles.shape[::-1], i32),
         V((padded, triangles.shape[0]), bf16),
-        V((2, padded, padded), bf16), V((3, vertices)),
-        V((2, planes * 48, vertices), bf16),
-        V((19, rows_x) + tile), V((planes, 3, 2) + tile),
+        V((padded, 2 * padded), bf16), V((3, vertices)),
+        V(((planes + 3) * 48, vertices), bf16), V((2 * depth, vertices), bf16),
+        V((3, 24, vertices)), V((3, depth, vertices), bf16),
+        V((19, rows_x) + tile), V((3, planes + 3) + tile),
     ]
-    for _ in ("receive", "send"):
-        scratch += [V((S, force_size(*d, rows_x)) + tile) for d in DIRS]
-        scratch += [V((S,) + p + tile) for p in pop_shapes]
-        scratch += [V((S, moment_size(*d, rows_x)) + tile) for d in DIRS]
-    scratch += [pltpu.SemaphoreType.DMA((S, 3, 8)), pltpu.SemaphoreType.DMA((S, 3, 8))]
+    tiles = sum(stage_sizes(rows_x, 2)[1], stage_sizes(rows_x, 2)[0])
+    scratch += [V((S, tiles) + tile)] * 2
+    scratch += [pltpu.SemaphoreType.DMA((S, 3))] * 2
     scratch += [pltpu.SemaphoreType.DMA((8,))]
     vmem = pl.BlockSpec(memory_space=pltpu.VMEM)
     hbm = pl.BlockSpec(memory_space=pltpu.HBM)

time: 42.2 us -> 39.8 us (0.943)
  Pallas kernels: 41.4 us -> 38.9 us
    pallas_call x1, Pallas kernels: 40.7 us -> 38.2 us  [local(): pl.pallas_call(functools.partial(body_kernel, mesh.shape['gx'], mesh.shap...]
where the time goes in v2:
time: 39.8 us; the launch traced here: 39.5 us
  Pallas kernels  38.9 us (98%)
  between operations  0.64 us (2%)
    pallas_call x1, Pallas kernels, local(): pl.pallas_call(functools.partial(body_kernel, mesh.shape['gx'], mesh.shap...  38.2 us

profile of v2, /device:TPU:1, one launch (start us, length us, event | category | flops | bytes accessed | tf_op | source)
XLA Modules:
  0.0 39.5 jit_solution(9329117155659607867)
XLA Ops:
  0.6 38.2 %shard_map.95 = (f32[19,4,8,128]{3,2,1,0:T(8,128)S(1)}, f32[3,2,768]{2,1,0:T(2,128)S(1)}) custom-call(f32[19,4,8,128]{3,2,1,0:T(8,128)} %pops_hbm.1, s32[4,8,128]{2,1,0:T(8,128)} %solid_hbm.1, s32[3,2,768]{2,1,0:T(2,128)} %bitcast.10, f32[3,2,768]{2,1,0:T(2,128)} %bitcast.11, f32[3,2,768]{2,1,0:T(2,128)} %bitcast.12, f32[2]{0:T(128)} %bitcast.13, ...), custom_call_target="tpu_custom_call" | custom-call | tf_op jit(solution)/shard_map/pallas_call | solution.py:636
  38.8 0.7 %shard_map.96 = (f32[19,4,8,128]{3,2,1,0:T(8,128)}, f32[3,2,768]{2,1,0:T(2,128)}) custom-call(f32[19,4,8,128]{3,2,1,0:T(8,128)S(1)} %get-tuple-element.6.pops_ref, f32[3,2,768]{2,1,0:T(2,128)S(1)} %get-tuple-element.7.offset_ref), custom_call_target="tpu_custom_call" | custom-call | tf_op jit(solution)/shard_map/pallas_call | solution.py:652

commit v3 on v2

--- a/solution.py
+++ b/solution.py
@@ -18,6 +18,7 @@
 LATTICE_WEIGHTS = [1.0 / 3.0] + [1.0 / 18.0] * 6 + [1.0 / 36.0] * 12
 RELAX = 0.8
 CHUNK = 256
+MASKS = (((0, 0.25), (1, 0.25), (2, 0.25), (3, 0.25)), ((1, 1.0), (3, -1.0)), ((2, 1.0), (0, -1.0)))
 XS = {s: [q for q in range(19) if VELOCITIES[q][0] == s] for s in (1, -1)}
 YS = {s: [q for q in range(19) if VELOCITIES[q][1] == s] for s in (1, -1)}
 CORNER = {(v[0], v[1]): q for q, v in enumerate(VELOCITIES) if v[0] and v[1]}
@@ -161,6 +162,10 @@
     return {0: n + packed(n, 2), 1: packed(n, 2), -1: packed(n, 1) + packed(n, 2)}[sy]
 
 
+def halved(sums):
+    return total_of([0.5 * x for x in sums if x is not None])
+
+
 def stage_sizes(rows_x, stage):
     force = [force_size(*d, rows_x) for d in DIRS]
     moment = [moment_size(*d, rows_x) for d in DIRS]
@@ -209,16 +214,17 @@
     parts = [slice(k, min(k + 256, faces)) for k in range(0, faces, 256)]
 
     def build_laplacian():
-        pairs = None
-        for cut in parts:
+        sums = [None, None]
+        for c, cut in enumerate(parts):
             part = mm(incidence[:, cut], incidence[:, cut], NT)
-            pairs = part if pairs is None else pairs + part
+            sums[c % 2] = part if sums[c % 2] is None else sums[c % 2] + part
+        pairs = halved(sums) * 2.0
         same = lax.broadcasted_iota(jnp.int32, pairs.shape, 0) == lax.broadcasted_iota(
             jnp.int32, pairs.shape, 1
         )
         lap_high, lap_low = split(jnp.where(same, -2.0 * pairs, pairs))
         lap[:, 0:padded] = lap_high
-        lap[:, padded:] = lap_low
+        lap[:, padded:] = -lap_low
 
     def flat(ref):
         return jnp.concatenate([ref[:, m, :] for m in range(slots)], axis=1)
@@ -239,7 +245,16 @@
     sub = lax.broadcasted_iota(jnp.int32, (8, depth), 0)
     distances = ((8, base_x, 0), (16, base_y, 8), (depth, base_z, 24))
 
-    for rows, base_row, start in distances:
+    short = lambda x: jnp.broadcast_to(x, (depth, vertices)).astype(jnp.int16)
+    cells = lax.broadcasted_iota(jnp.int32, (depth, vertices), 0) + 1
+    d = (short(cells) - short(base_z)) & short(jnp.int32(depth - 1))
+    unit = jnp.ones(d.shape, jnp.bfloat16)
+    for k, pairs in enumerate(MASKS):
+        value = 0.0 * unit
+        for j, weight in pairs:
+            value = jnp.where(d == short(jnp.int32(j)), weight * unit, value)
+        masks_z[k] = value
+    for rows, base_row, start in distances[:2]:
         d = distance(rows, base_row)
         fits = [
             jnp.where(d < 4, 0.25, 0.0),
@@ -247,10 +262,7 @@
             jnp.where(d == 2, 1.0, jnp.where(d == 0, -1.0, 0.0)),
         ]
         for k in range(3):
-            if rows == depth:
-                masks_z[k] = fits[k].astype(jnp.bfloat16)
-            else:
-                masks[k, start : start + rows, :] = fits[k]
+            masks[k, start : start + rows, :] = fits[k]
 
     def place(stage, d):
         start = stage_sizes(rows_x, stage)[0]
@@ -261,7 +273,7 @@
         part = pl.ds(start, size)
         return pltpu.make_async_remote_copy(
             src_ref=send_buf.at[step, part], dst_ref=recv_buf.at[step, part],
-            send_sem=send_sem.at[step, stage], recv_sem=recv_sem.at[step, stage],
+            send_sem=send_sem.at[0], recv_sem=recv_sem.at[step, stage],
             device_id=device, device_id_type=MESH,
         )
 
@@ -278,15 +290,18 @@
     def launch(step, stage):
         sends = [copy(step, stage, *place(stage, d), peer[d]) for d in range(8)]
 
-        @pl.when(iy % 2 == 1)
-        def _():
-            for d in (4, 6, 2, 5, 7, 3, 0, 1):
-                sends[d].start()
-
-        @pl.when(iy % 2 == 0)
-        def _():
-            for d in (5, 7, 3, 4, 6, 2, 0, 1):
-                sends[d].start()
+        for side in (0, 1):
+            for part in (0, 1):
+                near = 1 if side == 0 else -1
+                far = 1 if part == 1 else -1
+                first = (0, -near) if side == 0 else (-near, 0)
+                order = [(x, y) for y in (far, -far) for x in (*first, near)]
+                order += [(-near, 0), (near, 0)]
+
+                @pl.when((ix % 2 == side) & (iy % 2 == part))
+                def _(order=order):
+                    for name in order:
+                        sends[DIRS.index(name)].start()
 
     def arrive(step, stage):
         whole(step, stage).wait_recv()
@@ -338,8 +353,8 @@
             [strain[:, m * padded : (m + 1) * padded] for m in range(slots)], axis=0
         )
         if first:
-            pulled, pair = None, stacked(six)
-            for cut in parts:
+            sums, pair = [None, None], stacked(six)
+            for c, cut in enumerate(parts):
                 shape = (padded, cut.stop - cut.start)
                 ids = lax.broadcasted_iota(jnp.int32, shape, 0).astype(jnp.int16)
                 hit = None
@@ -354,13 +369,14 @@
                 part = mm(
                     jnp.concatenate([stacked(summed), ones], axis=0), incidence[:, cut], NT
                 )
-                pulled = part if pulled is None else pulled + part
+                sums[c % 2] = part if sums[c % 2] is None else sums[c % 2] + part
+            pulled = halved(sums) * 2.0
             count = pulled[6 * slots :]
             pulled = pulled[0 : 3 * slots] + pulled[3 * slots : 6 * slots]
             pulled = pulled - 3.0 * count * six
         else:
-            pulled = mm(stacked(six), lap[...], NN)
-            pulled = pulled[:, 0:padded] + pulled[:, padded:]
+            both = stacked(six)
+            pulled = mm(both, lap[:, 0:padded], NN) - mm(both, lap[:, padded:], NN)
             pulled = pulled[0 : 3 * slots] + pulled[3 * slots :]
         force_v = scale * jnp.concatenate(
             [pulled[3 * m : 3 * m + 3] for m in range(slots)], axis=1
@@ -588,12 +604,10 @@
     for m in range(slots):
         offset_out[:, m, :] = off[:, m * padded : (m + 1) * padded]
 
-    def drain(step, carry):
-        for stage in range(3):
-            whole(step, stage).wait_send()
-        return carry
-
-    lax.fori_loop(0, SUBSTEPS, drain, 0)
+    pltpu.make_async_remote_copy(
+        src_ref=send_buf, dst_ref=recv_buf, send_sem=send_sem.at[0], recv_sem=recv_sem.at[0, 0],
+        device_id=peer[0], device_id_type=MESH,
+    ).wait_send()
 
 
 def write_kernel(pops_ref, offset_ref, pops_out, offset_out, sem):
@@ -629,7 +643,7 @@
     ]
     tiles = sum(stage_sizes(rows_x, 2)[1], stage_sizes(rows_x, 2)[0])
     scratch += [V((S, tiles) + tile)] * 2
-    scratch += [pltpu.SemaphoreType.DMA((S, 3))] * 2
+    scratch += [pltpu.SemaphoreType.DMA((1,)), pltpu.SemaphoreType.DMA((S, 3))]
     scratch += [pltpu.SemaphoreType.DMA((8,))]
     vmem = pl.BlockSpec(memory_space=pltpu.VMEM)
     hbm = pl.BlockSpec(memory_space=pltpu.HBM)

time: 39.8 us -> 38.3 us (0.962)
  Pallas kernels: 38.9 us -> 37.5 us
    pallas_call x1, Pallas kernels: 38.2 us -> 36.8 us  [local(): pl.pallas_call(functools.partial(body_kernel, mesh.shape['gx'], mesh.shap...]
where the time goes in v3:
time: 38.3 us; the launch traced here: 38.2 us
  Pallas kernels  37.5 us (98%)
  between operations  0.64 us (2%)
    pallas_call x1, Pallas kernels, local(): pl.pallas_call(functools.partial(body_kernel, mesh.shape['gx'], mesh.shap...  36.8 us

profile of v3, /device:TPU:1, one launch (start us, length us, event | category | flops | bytes accessed | tf_op | source)
XLA Modules:
  0.0 38.2 jit_solution(8575348180881066470)
XLA Ops:
  0.6 36.8 %shard_map.95 = (f32[19,4,8,128]{3,2,1,0:T(8,128)S(1)}, f32[3,2,768]{2,1,0:T(2,128)S(1)}) custom-call(f32[19,4,8,128]{3,2,1,0:T(8,128)} %pops_hbm.1, s32[4,8,128]{2,1,0:T(8,128)} %solid_hbm.1, s32[3,2,768]{2,1,0:T(2,128)} %bitcast.10, f32[3,2,768]{2,1,0:T(2,128)} %bitcast.11, f32[3,2,768]{2,1,0:T(2,128)} %bitcast.12, f32[2]{0:T(128)} %bitcast.13, ...), custom_call_target="tpu_custom_call" | custom-call | tf_op jit(solution)/shard_map/pallas_call | solution.py:650
  37.4 0.7 %shard_map.96 = (f32[19,4,8,128]{3,2,1,0:T(8,128)}, f32[3,2,768]{2,1,0:T(2,128)}) custom-call(f32[19,4,8,128]{3,2,1,0:T(8,128)S(1)} %get-tuple-element.6.pops_ref, f32[3,2,768]{2,1,0:T(2,128)S(1)} %get-tuple-element.7.offset_ref), custom_call_target="tpu_custom_call" | custom-call | tf_op jit(solution)/shard_map/pallas_call | solution.py:666

commit v4 on v3

--- a/solution.py
+++ b/solution.py
@@ -157,9 +157,30 @@
     return n if sy == 0 else -(-n * (2 if sy == 1 else 1) // 8)
 
 
+def moment_names(sx, sy, rows_x, beyond):
+    names = []
+    for x in moment_planes(sx, rows_x):
+        ring = x in (-1, rows_x)
+        if beyond and sy == -1:
+            names += [(x, c) for c in ((0,) if ring else (0, 1, 3))]
+        else:
+            names += [(x, c) for c in ((0, 2, 3) if ring else (0, 1, 2, 3))]
+    return names
+
+
+def restore(part, sx, sy, rows_x):
+    for x in moment_planes(sx, rows_x):
+        ring = {-1: -1.0, rows_x: 1.0}.get(x)
+        if (x, 1) not in part:
+            part[x, 1] = ring * part[x, 0]
+        if (x, 2) not in part:
+            part[x, 2] = float(sy) * part[x, 0]
+    return part
+
+
 def moment_size(sx, sy, rows_x):
-    n = 4 * len(moment_planes(sx, rows_x))
-    return {0: n + packed(n, 2), 1: packed(n, 2), -1: packed(n, 1) + packed(n, 2)}[sy]
+    near, far = (len(moment_names(sx, sy, rows_x, k)) for k in (False, True))
+    return {0: near + packed(far, 2), 1: packed(near, 2), -1: packed(far, 1) + packed(near, 2)}[sy]
 
 
 def halved(sums):
@@ -287,21 +308,23 @@
     def got(step, stage, d, k):
         return recv_buf[step, place(stage, d)[0] + k]
 
-    def launch(step, stage):
-        sends = [copy(step, stage, *place(stage, d), peer[d]) for d in range(8)]
-
+    def launch_far(step, stage):
+        sends = {DIRS[d]: copy(step, stage, *place(stage, d), peer[d]) for d in range(2, 8)}
         for side in (0, 1):
             for part in (0, 1):
                 near = 1 if side == 0 else -1
                 far = 1 if part == 1 else -1
-                first = (0, -near) if side == 0 else (-near, 0)
-                order = [(x, y) for y in (far, -far) for x in (*first, near)]
-                order += [(-near, 0), (near, 0)]
+                turn = (0, -near, near) if side == 0 else (-near, near, 0)
+                order = [(x, y) for y in (far, -far) for x in turn]
 
                 @pl.when((ix % 2 == side) & (iy % 2 == part))
                 def _(order=order):
                     for name in order:
-                        sends[DIRS.index(name)].start()
+                        sends[name].start()
+
+    def launch_near(step, stage):
+        for d in (1, 0):
+            copy(step, stage, *place(stage, d), peer[d]).start()
 
     def arrive(step, stage):
         whole(step, stage).wait_recv()
@@ -385,7 +408,7 @@
         tiles_of = {}
 
         def spread_tiles(names, start):
-            half, sums = 8 * len(names), [None, None]
+            half, sums = 16 * -(-len(names) // 2), [None, None]
             for c, cut in enumerate(chunks):
                 for n in range(0, len(names), 2):
                     blocks = [
@@ -393,6 +416,8 @@
                         else pulled_x[a][x & 7 : (x & 7) + 1, cut] * table_y[0:8, cut]
                         for x, a, y in names[n : n + 2]
                     ]
+                    if len(blocks) == 1:
+                        blocks = blocks * 2
                     high, low = split(jnp.concatenate(blocks, axis=0))
                     row = start + 8 * n
                     spread[row : row + 16, cut] = high
@@ -408,7 +433,8 @@
         outer = [(None, a, y) for y in far_y for a in range(3)]
         outer += [(x, a, 0) for x in (rows_x, rows_x + 1, -1) for a in range(3)]
         spread_tiles(outer, 0)
-        for d, (sx, sy) in enumerate(DIRS):
+        def put_force(d):
+            sx, sy = DIRS[d]
             across = force_planes(sx, rows_x)
             if sy == 0:
                 tiles = [tiles_of[x, a, 0] for x in across for a in range(3)]
@@ -419,11 +445,15 @@
                 tiles = pack(tiles, across[0] & 7, len(across))
             for k, tile in enumerate(tiles):
                 put(step, 0, d, k, tile)
+
+        for d in range(8):
+            put_force(d)
         if first:
             pl.semaphore_wait(barrier, len(peer))
-        launch(step, 0)
-        spread_tiles([(x, a, 0) for x in range(rows_x) for a in range(3)], 16 * len(outer))
-
+        launch_far(step, 0)
+        launch_near(step, 0)
+        inner = [(x, a, 0) for x in range(rows_x) for a in range(3)]
+        spread_tiles(inner, 16 * len(outer))
         if first:
             build_laplacian()
             loads[6].wait()
@@ -503,9 +533,10 @@
             far = jnp.where(first_row, up, jnp.where(last_row, down, 0.0))
             for x in range(-1, rows_x + 1):
                 own[x, c] = (near[x + 1], far[x + 1])
-        for d, (sx, sy) in enumerate(DIRS):
-            names = [(x, c) for x in moment_planes(sx, rows_x) for c in range(4)]
-            near, far = [own[n][0] for n in names], [own[n][1] for n in names]
+        for d in (2, 3, 4, 5, 6, 7, 0, 1):
+            sx, sy = DIRS[d]
+            near = [own[n][0] for n in moment_names(sx, sy, rows_x, False)]
+            far = [own[n][1] for n in moment_names(sx, sy, rows_x, True)]
             if sy == 0:
                 tiles = near + pack(far, 7, 2)
             elif sy == 1:
@@ -514,7 +545,9 @@
                 tiles = pack(far, 7, 1) + pack(near, 0, 2)
             for k, tile in enumerate(tiles):
                 put(step, 1, d, k, tile)
-        launch(step, 1)
+            if d == 7:
+                launch_far(step, 1)
+        launch_near(step, 1)
         for n, sx in enumerate((1, -1)):
             edge = rows_x - 1 if sx == 1 else 0
             for k, q in enumerate(XS[sx]):
@@ -528,7 +561,8 @@
                 put(step, 2, 2 + n, x, rows_kept[x])
         for n, (sx, sy) in enumerate(DIRS[4:]):
             put(step, 2, 4 + n, 0, moved[CORNER[sx, sy]][rows_x - 1 if sx == 1 else 0])
-        launch(step, 2)
+        launch_far(step, 2)
+        launch_near(step, 2)
         arrive(step, 1)
         reach = [x for x in range(rows_x + 2)] + [-1]
         near = {(x, c): [] for x in reach for c in range(4)}
@@ -538,28 +572,27 @@
             far[name].append(b)
         two, edges, one = row_mask(0, 2, depth), row_mask(7, 2, depth), row_mask(7, 1, depth)
         for d, (sx, sy) in enumerate(DIRS):
-            names = [
-                (landing(x, sx, rows_x), c)
-                for x in moment_planes(sx, rows_x) for c in range(4)
-            ]
-            count = len(names)
+            names = moment_names(sx, sy, rows_x, False)
+            beyond = moment_names(sx, sy, rows_x, True)
             load = lambda k, d=d: got(step, 1, d, k)
             if sy == 0:
-                a = [load(k) for k in range(count)]
-                b = unpack(lambda k: load(count + k), count, 2)
+                a = [load(k) for k in range(len(names))]
+                b = unpack(lambda k: load(len(names) + k), len(beyond), 2)
                 b = [jnp.where(edges, t, 0.0) for t in b]
+                a, b = dict(zip(names, a)), dict(zip(beyond, b))
             elif sy == 1:
-                both_rows = unpack(load, count, 2)
-                a = [jnp.where(first_row, t, 0.0) for t in both_rows]
-                b = [jnp.where(last_row, t, 0.0) for t in both_rows]
+                both_rows = unpack(load, len(names), 2)
+                a = dict(zip(names, [jnp.where(first_row, t, 0.0) for t in both_rows]))
+                b = dict(zip(names, [jnp.where(last_row, t, 0.0) for t in both_rows]))
             else:
-                skip = packed(count, 1)
-                a = [jnp.where(one, t, 0.0) for t in unpack(load, count, 1)]
-                b = unpack(lambda k: load(skip + k), count, 2)
+                skip = packed(len(beyond), 1)
+                a = [jnp.where(one, t, 0.0) for t in unpack(load, len(beyond), 1)]
+                b = unpack(lambda k: load(skip + k), len(names), 2)
                 b = [jnp.where(two, t, 0.0) for t in b]
-            for name, p, r in zip(names, a, b):
-                near[name].append(p)
-                far[name].append(r)
+                a, b = dict(zip(beyond, a)), dict(zip(names, b))
+            for side, part in ((near, a), (far, b)):
+                for (x, c), tile in restore(part, sx, sy, rows_x).items():
+                    side[landing(x, sx, rows_x), c].append(tile)
         used = row_mask(7, 3, depth)
         count = len(reach)
         for i, x in enumerate(reach):
@@ -637,7 +670,7 @@
         pltpu.SMEM((slots,), f32), pltpu.SMEM((slots,), i32), V(triangles.shape[::-1], i32),
         V((padded, triangles.shape[0]), bf16),
         V((padded, 2 * padded), bf16), V((3, vertices)),
-        V(((planes + 3) * 48, vertices), bf16), V((2 * depth, vertices), bf16),
+        V(((planes + 3) * 48 + 32, vertices), bf16), V((2 * depth, vertices), bf16),
         V((3, 24, vertices)), V((3, depth, vertices), bf16),
         V((19, rows_x) + tile), V((3, planes + 3) + tile),
     ]

time: 38.3 us -> 38.4 us (level)
  no operation moved by 1% of the time
where the time goes in v4:
time: 38.4 us; the launch traced here: 38.1 us
  Pallas kernels  37.4 us (97%)
  between operations  0.64 us (2%)
    pallas_call x1, Pallas kernels, local(): pl.pallas_call(functools.partial(body_kernel, mesh.shape['gx'], mesh.shap...  36.7 us

profile of v4, /device:TPU:1, one launch (start us, length us, event | category | flops | bytes accessed | tf_op | source)
XLA Modules:
  0.0 38.1 jit_solution(10794074080469017572)
XLA Ops:
  0.6 36.7 %shard_map.95 = (f32[19,4,8,128]{3,2,1,0:T(8,128)S(1)}, f32[3,2,768]{2,1,0:T(2,128)S(1)}) custom-call(f32[19,4,8,128]{3,2,1,0:T(8,128)} %pops_hbm.1, s32[4,8,128]{2,1,0:T(8,128)} %solid_hbm.1, s32[3,2,768]{2,1,0:T(2,128)} %bitcast.10, f32[3,2,768]{2,1,0:T(2,128)} %bitcast.11, f32[3,2,768]{2,1,0:T(2,128)} %bitcast.12, f32[2]{0:T(128)} %bitcast.13, ...), custom_call_target="tpu_custom_call" | custom-call | tf_op jit(solution)/shard_map/pallas_call | solution.py:683
  37.3 0.7 %shard_map.96 = (f32[19,4,8,128]{3,2,1,0:T(8,128)}, f32[3,2,768]{2,1,0:T(2,128)}) custom-call(f32[19,4,8,128]{3,2,1,0:T(8,128)S(1)} %get-tuple-element.6.pops_ref, f32[3,2,768]{2,1,0:T(2,128)S(1)} %get-tuple-element.7.offset_ref), custom_call_target="tpu_custom_call" | custom-call | tf_op jit(solution)/shard_map/pallas_call | solution.py:699
